TPU v7x, 32 devices: a whole 2x2x4 slice. The times are simulated.
32 devices in a mesh: rows: 8 (over y, x, core), rhs: 4 (over z).
Axes of the slice: x: 2, y: 2, z: 4, core: 2. Of those that a mesh axis runs over, the one named last changes fastest.
Arguments:
- sources: bfloat16 [32768, 2048], P('rows', 'rhs'), may hold values from -6 to 6
- near_blocks: bfloat16 [128, 3, 256, 256], P('rows'), may hold values from -0.21875 to 0.21875
- near_list: int32 [128, 3], P('rows'), may hold values from 0 to 127, as said below
- source_basis: bfloat16 [128, 256, 32], P('rows'), may hold values from -0.375 to 0.375
- target_basis: bfloat16 [128, 256, 32], P('rows'), may hold values from -0.375 to 0.375
- transfer_fine: bfloat16 [224, 32, 32], P('rows'), may hold values from -0.875 to 0.875
- transfer_coarse: bfloat16 [32, 32, 32], P('rhs'), may hold values from -0.875 to 0.875
- couple_fine: bfloat16 [224, 3, 32, 32], P('rows'), may hold values from -0.625 to 0.625
- couple_coarse: bfloat16 [32, 3, 32, 32], P('rhs'), may hold values from -0.625 to 0.625
- far_fine: int32 [224, 3], P('rows'), may hold values from 0 to 127, as said below
- far_coarse: int32 [32, 3], replicated, may hold values from -1 to 15, as said below
Outputs:
- potentials: bfloat16 [32768, 2048], P('rows', 'rhs')
Inputs may be any that keep to these rules, and one draw needn't show every extreme that they name: `near_list`: row t lists the leaf clusters t - 1, t and t + 1 modulo 128 in some order. `far_fine`: row d * 28 + o + i belongs to cluster d * m + i of the level with n = m * 8 clusters, where (o, m) is (0, 16), (16, 8) or (24, 4). It lists, in some order, the three clusters of that level that are children of the cyclic neighbours of the cluster's parent and not cyclic neighbours of the cluster: for cluster j with parent p = j // 2, the clusters 2p - 2, 2p + 2, 2p + 3 if j is even and 2p - 2, 2p - 1, 2p + 3 if j is odd, modulo n. `far_coarse`: row n + j for n = 8, 16, ..., 16 lists, in some order, the three far clusters of cluster j of the level with n clusters by the rule of far_fine. Row 4 + j holds (j + 2) modulo 4 in slot 0 and -1 in slots 1 and 2. Rows 0 to 3 hold -1.
All inputs are finite; a program needn't handle non-finite values.
Results may differ from a plain program's by a relative error of at most 0.012.
Values may be sent and summed in bfloat16 or wider, within the bound.
A program may use at most 128 MiB of HBM per device.

v0:
```python
import jax
import jax.numpy as jnp
from jax import lax
from jax.sharding import PartitionSpec as P


def padded_2(cells, sides, width):
    for axis, dim in sides:
        count = lax.axis_size(axis)
        head = lax.slice_in_dim(cells, 0, width, axis=dim)
        tail = lax.slice_in_dim(cells, cells.shape[dim] - width, cells.shape[dim], axis=dim)
        cells = jnp.concatenate(
            [
                lax.ppermute(tail, axis, [(i, (i + 1) % count) for i in range(count)]),
                cells,
                lax.ppermute(head, axis, [((i + 1) % count, i) for i in range(count)]),
            ],
            axis=dim,
        )
    return cells


def couple_masked(moments, blocks, partners):
    valid = partners >= 0
    picked = moments[jnp.maximum(partners, 0)]
    picked = jnp.where(valid[:, :, None, None], picked, jnp.zeros_like(picked))
    return jnp.einsum("nsab,nsbr->nar", blocks, picked, preferred_element_type=jnp.float32)


def routed_blocks(blocks, offset, wanted):
    chosen = jnp.zeros_like(blocks[:, 0])
    for slot in range(3):
        match = (offset[:, slot] == wanted)[:, None, None]
        chosen = jnp.where(match, blocks[:, slot], chosen)
    return chosen


def couple_window(moments, blocks, partners, position, row_count):
    clusters = moments.shape[0]
    level_size = clusters * row_count
    window = padded_2(moments, (("rows", 0),), 3)
    targets = position * clusters + jnp.arange(clusters, dtype=jnp.int32)
    offset = (partners - targets[:, None] + level_size // 2) % level_size - level_size // 2
    coupled = jnp.zeros((clusters, moments.shape[1], moments.shape[2]), jnp.float32)
    for wanted in (-3, -2, 2, 3):
        chosen = routed_blocks(blocks, offset, wanted)
        shifted = window[3 + wanted : 3 + wanted + clusters]
        coupled = coupled + jnp.einsum(
            "nab,nbr->nar", chosen, shifted, preferred_element_type=jnp.float32
        )
    return coupled


def lift(moments, transfer):
    clusters, rank, width = moments.shape
    product = jnp.einsum("nab,nar->nbr", transfer, moments, preferred_element_type=jnp.float32)
    return product.reshape(clusters // 2, 2, rank, width).sum(axis=1).astype(jnp.bfloat16)


def lower(parent, transfer, coupled):
    spread = jnp.repeat(parent, 2, axis=0)
    carried = jnp.einsum("nab,nbr->nar", transfer, spread, preferred_element_type=jnp.float32)
    return (coupled + carried).astype(jnp.bfloat16)


def coarse_pass(moments, transfer_all, couple_all, far_all):
    clusters = moments.shape[0]
    depth = clusters.bit_length() - 3
    upward = [moments]
    for step in range(depth):
        moments = lift(moments, transfer_all[clusters : 2 * clusters])
        clusters = clusters // 2
        upward.append(moments)
    downward = moments
    for step in range(depth + 1):
        coupled = couple_masked(
            upward[depth - step],
            couple_all[clusters : 2 * clusters],
            far_all[clusters : 2 * clusters],
        )
        if step == 0:
            downward = coupled.astype(jnp.bfloat16)
        else:
            downward = lower(downward, transfer_all[clusters : 2 * clusters], coupled)
        clusters = clusters * 2
    return downward


def body(
    sources,
    near_blocks,
    near_list,
    source_basis,
    target_basis,
    transfer_fine,
    transfer_coarse,
    couple_fine,
    couple_coarse,
    far_fine,
    far_coarse,
):
    count = near_blocks.shape[0]
    leaf = near_blocks.shape[2]
    width = sources.shape[1]
    row_count = lax.axis_size("rows")
    position = lax.axis_index("rows")
    all_leaves = count * row_count
    padded = padded_2(sources, (("rows", 0),), leaf)
    neighbours = padded.reshape(count + 2, leaf, width)
    targets = position * count + jnp.arange(count, dtype=jnp.int32)
    offset = (near_list - targets[:, None] + all_leaves // 2) % all_leaves - all_leaves // 2
    near_part = jnp.zeros((count, leaf, width), jnp.float32)
    for wanted in (-1, 0, 1):
        chosen = routed_blocks(near_blocks, offset, wanted)
        shifted = neighbours[1 + wanted : 1 + wanted + count]
        near_part = near_part + jnp.einsum(
            "npq,nqr->npr", chosen, shifted, preferred_element_type=jnp.float32
        )
    shaped = sources.reshape(count, leaf, width)
    moments = jnp.einsum(
        "npk,npr->nkr", source_basis, shaped, preferred_element_type=jnp.float32
    ).astype(jnp.bfloat16)
    level_counts = [count, count // 2, count // 4]
    firsts = [0, count, count + count // 2]
    upward = [moments]
    for level in range(3):
        moments = lift(moments, transfer_fine[firsts[level] : firsts[level] + level_counts[level]])
        upward.append(moments)
    tables = (
        lax.all_gather(transfer_coarse, "rhs", axis=0, tiled=True),
        lax.all_gather(couple_coarse, "rhs", axis=0, tiled=True),
    )
    whole = lax.all_gather(moments, "rows", axis=0, tiled=True)
    result = coarse_pass(whole, tables[0], tables[1], far_coarse)
    parents = lax.dynamic_slice_in_dim(result, 2 * position, 2, 0)
    downward = parents
    for level in (2, 1, 0):
        first = firsts[level]
        last = first + level_counts[level]
        coupled = couple_window(
            upward[level], couple_fine[first:last], far_fine[first:last], position, row_count
        )
        downward = lower(downward, transfer_fine[first:last], coupled)
    far_part = jnp.einsum(
        "npk,nkr->npr", target_basis, downward, preferred_element_type=jnp.float32
    )
    return (far_part + near_part).astype(jnp.bfloat16).reshape(count * leaf, width)


def solution(mesh):
    in_specs = (
        P("rows", "rhs"),
        P("rows", None, None, None),
        P("rows", None),
        P("rows", None, None),
        P("rows", None, None),
        P("rows", None, None),
        P("rhs", None, None),
        P("rows", None, None, None),
        P("rhs", None, None, None),
        P("rows", None),
        P(),
    )
    out_specs = P("rows", "rhs")
    return jax.shard_map(body, mesh=mesh, in_specs=in_specs, out_specs=out_specs, check_vma=False)
```

profile of v0, /device:TPU:0, one launch (start us, length us, event | category | flops | bytes accessed | tf_op | source)
XLA Modules:
  0.0 131.6 jit_solution(1176060238905325471)
XLA Ops:
  0.0 3.1 %convolution_convert_fusion = bf16[16,32,512]{2,1,0:T(8,128)(2,1)S(1)} fusion(bf16[16,256,32]{1,2,0:T(8,128)(2,1)} %param.14, bf16[16,256,512]{2,1,0:T(8,128)(2,1)} %bitcast.394), kind=kOutput, calls=%fused_computation.53 | convolution fusion | flops 134479872 | bytes 4980736 | tf_op jit(solution)/shard_map/npk,npr->nkr/dot_general | solution.py:120
  3.2 0.7 fusion.309
  3.9 0.5 collective-permute-start
  4.4 2.9 %collective-permute-start.1 = (bf16[3,32,512]{2,1,0:T(8,128)(2,1)}, bf16[3,32,512]{2,1,0:T(8,128)(2,1)}, u32[]{:S(2)}, u32[]{:S(2)}) collective-permute-start(bf16[3,32,512]{2,1,0:T(8,128)(2,1)} %get-tuple-element.10), channel_id=1, source_target_pairs={{4,0},{8,4},{12,8},{16,12},{20,16},{24,20},{28,24},{0,28},{5,1},{9... | collective-permute-start | bytes 294920 | tf_op jit(solution)/shard_map/ppermute | solution.py:16
  7.3 0.3 bitcast_reduce_fusion.1
  7.6 0.3 bitcast_reduce_fusion.3
  7.9 0.7 fusion.311
  8.6 2.6 %collective-permute-start.5 = (bf16[3,32,512]{2,1,0:T(8,128)(2,1)}, bf16[3,32,512]{2,1,0:T(8,128)(2,1)}, u32[]{:S(2)}, u32[]{:S(2)}) collective-permute-start(bf16[3,32,512]{2,1,0:T(8,128)(2,1)} %get-tuple-element.14), channel_id=1, source_target_pairs={{4,0},{8,4},{12,8},{16,12},{20,16},{24,20},{28,24},{0,28},{5,1},{9... | collective-permute-start | bytes 294920 | tf_op jit(solution)/shard_map/ppermute | solution.py:16
  11.2 0.7 fusion.310
  12.4 0.2 bitcast_reduce_fusion.4
  12.6 1.9 %fusion.308 = (bf16[256,512]{1,0:T(8,128)(2,1)}, bf16[256,512]{1,0:T(8,128)(2,1)}) fusion(bf16[4096,512]{1,0:T(8,128)(2,1)} %param.11), kind=kLoop, calls=%fused_computation.393 | loop fusion | bytes 1048576 | tf_op jit(solution)/shard_map/slice | solution.py:10
  14.7 0.7 copy.64
  15.9 0.6 compare_bitcast_fusion.2
  16.6 0.6 compare_bitcast_fusion.32
  17.2 0.6 compare_bitcast_fusion.20
  18.0 14.9 %all_gather.11 = bf16[32,32,32]{2,1,0:T(8,128)(2,1)S(1)} all-gather(bf16[8,32,32]{2,1,0:T(8,128)(2,1)S(1)} %copy-done.7), channel_id=1, replica_groups=mesh['rows'=8,'rhs'=4] {'rhs'}, dimensions={0}, use_global_device_ids=true | all-gather | bytes 81920 | tf_op jit(solution)/shard_map/all_gather | solution.py:130
  32.9 9.8 %all_gather.9 = bf16[16,32,512]{2,1,0:T(8,128)(2,1)S(1)} all-gather(bf16[2,32,512]{2,1,0:T(8,128)(2,1)S(1)} %bitcast_reduce_fusion.4), channel_id=1, replica_groups=mesh['rows'=8,'rhs'=4] {'rows'}, dimensions={0}, use_global_device_ids=true | all-gather | bytes 589824 | tf_op jit(solution)/shard_map/all_gather | solution.py:133
  42.7 0.3 bitcast_reduce_fusion
  43.1 0.3 bitcast_reduce_fusion.2
  43.4 0.6 gather_fusion.1
  44.0 20.9 %all_gather.10 = bf16[32,3,32,32]{3,2,1,0:T(8,128)(2,1)} all-gather(bf16[8,3,32,32]{3,2,1,0:T(8,128)(2,1)} %param.19), channel_id=1, replica_groups=mesh['rows'=8,'rhs'=4] {'rhs'}, dimensions={0}, use_global_device_ids=true | all-gather | bytes 245760 | tf_op jit(solution)/shard_map/all_gather | solution.py:131
  64.8 1.3 %gather_fusion.2 = bf16[12,32,512]{2,1,0:T(8,128)(2,1)} fusion(bf16[4,32,512]{2,1,0:T(8,128)(2,1)S(1)} %bitcast_reduce_fusion.2, s32[1024]{0:T(1024)S(1)} %pad_clamp_fusion), kind=kCustom, calls=%fused_computation.2 | custom fusion | bytes 786480 | tf_op jit(solution)/shard_map/gather | solution.py:25
  66.2 1.2 convolution_bitcast_fusion.2
  67.4 1.3 fusion.61
  69.0 1.2 fusion.134
  70.3 0.7 gather_fusion
  70.9 1.6 %fusion.42 = f32[16,512,32]{1,2,0:T(8,128)S(1)} fusion(bf16[16,3,32,512]{3,2,1,0:T(8,128)(2,1)S(1)} %bitcast.400, pred[16,3]{1,0:T(8,128)(4,1)} %copy.64, bf16[32,3,32,32]{3,2,1,0:T(8,128)(2,1)} %all_gather.10), kind=kOutput, calls=%fused_computation.46 | convolution fusion | flops 51118080 | bytes 3016704 | tf_op jit(solution)/shard_map/nsab,nsbr->nar/dot_general | solution.py:27
  72.5 0.9 fusion.159
  73.7 7.6 %fusion.7 = f32[16,256,512]{2,1,0:T(8,128)} fusion(bf16[16,256,512]{2,1,0:T(8,128)(2,1)S(1)} %bitcast.395, pred[16]{0:T(512)(128)(4,1)} %get-tuple-element.19, pred[16]{0:T(512)(128)(4,1)} %get-tuple-element.17, pred[16]{0:T(512)(128)(4,1)} %get-tuple-element.16, bf16[16,3,256,256]{3,2,1,0:T(8,128)(2,1)} %param.12), kind=kOutput, calls=%fused_computation.15 | convolution fusion | flops 1076887552 | bytes 18874416 | tf_op jit(solution)/shard_map/npq,nqr->npr/dot_general | solution.py:116
  81.4 0.4 collective-permute-start.3
  81.8 1.1 fusion.99
  83.0 1.1 fusion.94
  84.1 1.3 collective-permute-start.7
  85.4 1.1 fusion.101
  86.4 1.2 fusion.59
  87.8 0.2 collective-permute-start.6
  88.1 0.3 fusion.87
  88.4 0.3 fusion.83
  88.7 1.1 fusion.89
  89.8 1.2 fusion.53
  91.1 0.3 convolution_bitcast_fusion
  91.4 1.2 fusion.74
  92.6 2.2 %fusion.69 = f32[16,32,512]{2,1,0:T(8,128)} fusion(bf16[16,32,512]{2,1,0:T(8,128)(2,1)S(1)} %convolution_convert_fusion, bf16[3,32,512]{2,1,0:T(8,128)(2,1)} %collective-permute-done.1, pred[16]{0:T(512)(128)(4,1)S(1)} %get-tuple-element.32, pred[16]{0:T(512)(128)(4,1)S(1)} %get-tuple-element.29, pred[16]{0:T(512)(128)(4,1)S(1)} %get-tuple-element.26, ...), kind=kOutput, calls=%fused_computation.87 | convolution fusion | flops 17088512 | bytes 2065920 | tf_op jit(solution)/shard_map/nab,nbr->nar/dot_general | solution.py:48
  94.8 2.2 %fusion.76 = f32[16,32,512]{2,1,0:T(8,128)} fusion(bf16[16,32,512]{2,1,0:T(8,128)(2,1)S(1)} %convolution_convert_fusion, bf16[3,32,512]{2,1,0:T(8,128)(2,1)} %collective-permute-done, pred[16]{0:T(512)(128)(4,1)S(1)} %get-tuple-element.31, pred[16]{0:T(512)(128)(4,1)S(1)} %get-tuple-element.28, pred[16]{0:T(512)(128)(4,1)S(1)} %get-tuple-element.25, ...), kind=kOutput, calls=%fused_computation.93 | convolution fusion | flops 17088512 | bytes 2065920 | tf_op jit(solution)/shard_map/nab,nbr->nar/dot_general | solution.py:48
  96.9 6.6 %fusion.52 = f32[16,512,256]{1,2,0:T(8,128)} fusion(bf16[16,256,32]{1,2,0:T(8,128)(2,1)S(1)} %copy-done, f32[16,32,512]{2,1,0:T(8,128)S(1)} %convolution_bitcast_fusion, f32[16,32,512]{2,1,0:T(8,128)S(1)} %fusion.74, f32[16,32,512]{2,1,0:T(8,128)} %fusion.69, f32[16,32,512]{2,1,0:T(8,128)} %fusion.76, bf16[3,32,512]{2,1,0:T(8,128)(2,1)} %collective-permute-done, ...), kind=kOutput, calls=%fused_computation.61 | convolution fusion | flops 152616960 | bytes 13860912 | tf_op jit(solution)/shard_map/npk,nkr->npr/dot_general | solution.py:144
  103.5 5.0 %pad_maximum_fusion = (bf16[4096,512]{1,0:T(8,128)(2,1)}, bf16[4096,512]{1,0:T(8,128)(2,1)S(1)}) fusion(bf16[256,512]{1,0:T(8,128)(2,1)S(1)} %collective-permute-done.7, bf16[4096,512]{1,0:T(8,128)(2,1)} %param.11, bf16[256,512]{1,0:T(8,128)(2,1)} %collective-permute-done.6), kind=kLoop, calls=%fused_computation.5 | loop fusion | flops 16777216 | bytes 13107200 | tf_op jit(solution)/shard_map/concatenate | solution.py:12
  108.6 7.6 %fusion.3 = f32[16,256,512]{2,1,0:T(8,128)} fusion(bf16[16,256,512]{2,1,0:T(8,128)(2,1)S(1)} %bitcast.397, pred[16]{0:T(512)(128)(4,1)S(1)} %copy-done.24, pred[16]{0:T(512)(128)(4,1)S(1)} %copy-done.25, pred[16]{0:T(512)(128)(4,1)S(1)} %copy-done.26, bf16[16,3,256,256]{3,2,1,0:T(8,128)(2,1)} %param.12), kind=kOutput, calls=%fused_computation.12 | convolution fusion | flops 1076887552 | bytes 18874416 | tf_op jit(solution)/shard_map/npq,nqr->npr/dot_general | solution.py:116
  116.3 15.3 %fusion = bf16[16,256,512]{2,1,0:T(8,128)(2,1)} fusion(f32[16,512,256]{1,2,0:T(8,128)} %fusion.52, f32[16,256,512]{2,1,0:T(8,128)} %fusion.3, f32[16,256,512]{2,1,0:T(8,128)} %fusion.7, bf16[16,256,512]{2,1,0:T(8,128)(2,1)} %bitcast.396, pred[16]{0:T(512)(128)(4,1)S(1)} %copy-done.23, pred[16]{0:T(512)(128)(4,1)S(1)} %copy-done.22, ...), kind=kOutput, calls=%fused_computation.4 | convolution fusion | flops 1085276160 | bytes 39845936 | tf_op jit(solution)/shard_map/npq,nqr->npr/dot_general | solution.py:116
  (102 shorter events, 2.2 us)
Async XLA Ops:
  0.0 96.9 %copy-start = (bf16[16,256,32]{1,2,0:T(8,128)(2,1)S(1)}, bf16[16,256,32]{1,2,0:T(8,128)(2,1)}, u32[]{:S(2)}) copy-start(bf16[16,256,32]{1,2,0:T(8,128)(2,1)} %param.15) | copy-start | bytes 786436
  0.0 7.3 %copy-start.3 = (bf16[28,32,32]{2,1,0:T(8,128)(2,1)S(1)}, bf16[28,32,32]{2,1,0:T(8,128)(2,1)}, u32[]{:S(2)}) copy-start(bf16[28,32,32]{2,1,0:T(8,128)(2,1)} %param.16) | copy-start | bytes 172036
  0.0 11.9 %copy-start.6 = (s32[32,3]{0,1:T(4,128)S(1)}, s32[32,3]{0,1:T(4,128)}, u32[]{:S(2)}) copy-start(s32[32,3]{0,1:T(4,128)} %param.21) | copy-start | bytes 1156
  0.0 15.4 %copy-start.8 = (s32[28,3]{0,1:T(4,128)S(1)}, s32[28,3]{0,1:T(4,128)}, u32[]{:S(2)}) copy-start(s32[28,3]{0,1:T(4,128)} %param.20) | copy-start | bytes 1012
  0.0 15.9 %copy-start.17 = (s32[16,3]{0,1:T(4,128)S(1)}, s32[16,3]{0,1:T(4,128)}, u32[]{:S(2)}) copy-start(s32[16,3]{0,1:T(4,128)} %param.13) | copy-start | bytes 580
  0.0 18.0 %copy-start.7 = (bf16[8,32,32]{2,1,0:T(8,128)(2,1)S(1)}, bf16[8,32,32]{2,1,0:T(8,128)(2,1)}, u32[]{:S(2)}) copy-start(bf16[8,32,32]{2,1,0:T(8,128)(2,1)} %param.17) | copy-start | bytes 49156
  3.9 90.9 %collective-permute-start = (bf16[3,32,512]{2,1,0:T(8,128)(2,1)}, bf16[3,32,512]{2,1,0:T(8,128)(2,1)}, u32[]{:S(2)}, u32[]{:S(2)}) collective-permute-start(bf16[3,32,512]{2,1,0:T(8,128)(2,1)} %get-tuple-element.9), channel_id=1, source_target_pairs={{0,4},{4,8},{8,12},{12,16},{16,20},{20,24},{24,28},{28,0},{1,5},{5... | collective-permute-start | bytes 294920 | tf_op jit(solution)/shard_map/ppermute | solution.py:14
  4.4 87.0 %collective-permute-start.1 = (bf16[3,32,512]{2,1,0:T(8,128)(2,1)}, bf16[3,32,512]{2,1,0:T(8,128)(2,1)}, u32[]{:S(2)}, u32[]{:S(2)}) collective-permute-start(bf16[3,32,512]{2,1,0:T(8,128)(2,1)} %get-tuple-element.10), channel_id=1, source_target_pairs={{4,0},{8,4},{12,8},{16,12},{20,16},{24,20},{28,24},{0,28},{5,1},{9... | collective-permute-start | bytes 294920 | tf_op jit(solution)/shard_map/ppermute | solution.py:16
  8.6 75.5 %collective-permute-start.4 = (bf16[3,32,512]{2,1,0:T(8,128)(2,1)}, bf16[3,32,512]{2,1,0:T(8,128)(2,1)}, u32[]{:S(2)}, u32[]{:S(2)}) collective-permute-start(bf16[3,32,512]{2,1,0:T(8,128)(2,1)} %get-tuple-element.13), channel_id=1, source_target_pairs={{0,4},{4,8},{8,12},{12,16},{16,20},{20,24},{24,28},{28,0},{1,5},{5... | collective-permute-start | bytes 294920 | tf_op jit(solution)/shard_map/ppermute | solution.py:14
  8.6 72.8 %collective-permute-start.5 = (bf16[3,32,512]{2,1,0:T(8,128)(2,1)}, bf16[3,32,512]{2,1,0:T(8,128)(2,1)}, u32[]{:S(2)}, u32[]{:S(2)}) collective-permute-start(bf16[3,32,512]{2,1,0:T(8,128)(2,1)} %get-tuple-element.14), channel_id=1, source_target_pairs={{4,0},{8,4},{12,8},{16,12},{20,16},{24,20},{28,24},{0,28},{5,1},{9... | collective-permute-start | bytes 294920 | tf_op jit(solution)/shard_map/ppermute | solution.py:16
  11.9 76.8 %collective-permute-start.2 = (bf16[3,32,512]{2,1,0:T(8,128)(2,1)}, bf16[3,32,512]{2,1,0:T(8,128)(2,1)}, u32[]{:S(2)}, u32[]{:S(2)}) collective-permute-start(bf16[3,32,512]{2,1,0:T(8,128)(2,1)} %get-tuple-element.11), channel_id=1, source_target_pairs={{0,4},{4,8},{8,12},{12,16},{16,20},{20,24},{24,28},{28,0},{1,5},{5... | collective-permute-start | bytes 294920 | tf_op jit(solution)/shard_map/ppermute | solution.py:14
  70.9 2.7 %copy-start.2 = (bf16[4096,512]{1,0:T(8,128)(2,1)S(1)}, bf16[4096,512]{1,0:T(8,128)(2,1)}, u32[]{:S(2)}) copy-start(bf16[4096,512]{1,0:T(8,128)(2,1)} %param.11) | copy-start | bytes 12582916
  73.6 7.8 %copy-start.5 = (bf16[3,32,512]{2,1,0:T(8,128)(2,1)S(1)}, bf16[3,32,512]{2,1,0:T(8,128)(2,1)}, u32[]{:S(2)}) copy-start(bf16[3,32,512]{2,1,0:T(8,128)(2,1)} %get-tuple-element.12) | copy-start | bytes 294916
  73.6 8.2 %copy-start.4 = (bf16[28,3,32,32]{3,2,1,0:T(8,128)(2,1)S(1)}, bf16[28,3,32,32]{3,2,1,0:T(8,128)(2,1)}, u32[]{:S(2)}) copy-start(bf16[28,3,32,32]{3,2,1,0:T(8,128)(2,1)} %param.18) | copy-start | bytes 516100
  73.7 8.2 %copy-start.14 = (pred[4]{0:T(512)(128)(4,1)S(1)}, pred[4]{0:T(512)(128)(4,1)}, u32[]{:S(2)}) copy-start(pred[4]{0:T(512)(128)(4,1)} %get-tuple-element.51) | copy-start | bytes 16
  73.7 8.2 %copy-start.15 = (pred[4]{0:T(512)(128)(4,1)S(1)}, pred[4]{0:T(512)(128)(4,1)}, u32[]{:S(2)}) copy-start(pred[4]{0:T(512)(128)(4,1)} %get-tuple-element.54) | copy-start | bytes 16
  73.7 8.2 %copy-start.16 = (pred[4]{0:T(512)(128)(4,1)S(1)}, pred[4]{0:T(512)(128)(4,1)}, u32[]{:S(2)}) copy-start(pred[4]{0:T(512)(128)(4,1)} %get-tuple-element.57) | copy-start | bytes 16
  73.7 9.3 %copy-start.11 = (pred[4]{0:T(512)(128)(4,1)S(1)}, pred[4]{0:T(512)(128)(4,1)}, u32[]{:S(2)}) copy-start(pred[4]{0:T(512)(128)(4,1)} %get-tuple-element.50) | copy-start | bytes 16
  73.7 9.3 %copy-start.12 = (pred[4]{0:T(512)(128)(4,1)S(1)}, pred[4]{0:T(512)(128)(4,1)}, u32[]{:S(2)}) copy-start(pred[4]{0:T(512)(128)(4,1)} %get-tuple-element.53) | copy-start | bytes 16
  73.7 9.3 %copy-start.13 = (pred[4]{0:T(512)(128)(4,1)S(1)}, pred[4]{0:T(512)(128)(4,1)}, u32[]{:S(2)}) copy-start(pred[4]{0:T(512)(128)(4,1)} %get-tuple-element.56) | copy-start | bytes 16
  73.7 11.7 %copy-start.9 = (pred[4]{0:T(512)(128)(4,1)S(1)}, pred[4]{0:T(512)(128)(4,1)}, u32[]{:S(2)}) copy-start(pred[4]{0:T(512)(128)(4,1)} %get-tuple-element.52) | copy-start | bytes 16
  73.7 11.6 %copy-start.10 = (pred[4]{0:T(512)(128)(4,1)S(1)}, pred[4]{0:T(512)(128)(4,1)}, u32[]{:S(2)}) copy-start(pred[4]{0:T(512)(128)(4,1)} %get-tuple-element.55) | copy-start | bytes 16
  81.3 7.0 %copy-start.27 = (pred[8]{0:T(512)(128)(4,1)S(1)}, pred[8]{0:T(512)(128)(4,1)}, u32[]{:S(2)}) copy-start(pred[8]{0:T(512)(128)(4,1)} %get-tuple-element.38) | copy-start | bytes 28
  81.3 7.0 %copy-start.28 = (pred[8]{0:T(512)(128)(4,1)S(1)}, pred[8]{0:T(512)(128)(4,1)}, u32[]{:S(2)}) copy-start(pred[8]{0:T(512)(128)(4,1)} %get-tuple-element.41) | copy-start | bytes 28
  81.3 7.1 %copy-start.29 = (pred[8]{0:T(512)(128)(4,1)S(1)}, pred[8]{0:T(512)(128)(4,1)}, u32[]{:S(2)}) copy-start(pred[8]{0:T(512)(128)(4,1)} %get-tuple-element.44) | copy-start | bytes 28
  81.3 8.5 %copy-start.18 = (pred[8]{0:T(512)(128)(4,1)S(1)}, pred[8]{0:T(512)(128)(4,1)}, u32[]{:S(2)}) copy-start(pred[8]{0:T(512)(128)(4,1)} %get-tuple-element.36) | copy-start | bytes 28
  81.3 8.5 %copy-start.19 = (pred[8]{0:T(512)(128)(4,1)S(1)}, pred[8]{0:T(512)(128)(4,1)}, u32[]{:S(2)}) copy-start(pred[8]{0:T(512)(128)(4,1)} %get-tuple-element.46) | copy-start | bytes 28
  81.4 8.5 %copy-start.20 = (pred[8]{0:T(512)(128)(4,1)S(1)}, pred[8]{0:T(512)(128)(4,1)}, u32[]{:S(2)}) copy-start(pred[8]{0:T(512)(128)(4,1)} %get-tuple-element.47) | copy-start | bytes 28
  81.4 6.4 %collective-permute-start.3 = (bf16[3,32,512]{2,1,0:T(8,128)(2,1)S(1)}, bf16[3,32,512]{2,1,0:T(8,128)(2,1)S(1)}, u32[]{:S(2)}, u32[]{:S(2)}) collective-permute-start(bf16[3,32,512]{2,1,0:T(8,128)(2,1)S(1)} %copy-done.5), channel_id=1, source_target_pairs={{4,0},{8,4},{12,8},{16,12},{20,16},{24,20},{28,24},{0,28},{5,1},{9... | collective-permute-start | bytes 294920 | tf_op jit(solution)/shard_map/ppermute | solution.py:16
  84.1 19.4 %collective-permute-start.7 = (bf16[256,512]{1,0:T(8,128)(2,1)}, bf16[256,512]{1,0:T(8,128)(2,1)S(1)}, u32[]{:S(2)}, u32[]{:S(2)}) collective-permute-start(bf16[256,512]{1,0:T(8,128)(2,1)} %get-tuple-element.7), channel_id=1, source_target_pairs={{4,0},{8,4},{12,8},{16,12},{20,16},{24,20},{28,24},{0,28},{5,1},{9... | collective-permute-start | bytes 786440 | tf_op jit(solution)/shard_map/ppermute | solution.py:16
  87.8 15.7 %collective-permute-start.6 = (bf16[256,512]{1,0:T(8,128)(2,1)}, bf16[256,512]{1,0:T(8,128)(2,1)}, u32[]{:S(2)}, u32[]{:S(2)}) collective-permute-start(bf16[256,512]{1,0:T(8,128)(2,1)} %get-tuple-element.8), channel_id=1, source_target_pairs={{0,4},{4,8},{8,12},{12,16},{16,20},{20,24},{24,28},{28,0},{1,5},{5... | collective-permute-start | bytes 786440 | tf_op jit(solution)/shard_map/ppermute | solution.py:14
  103.5 5.1 %copy-start.24 = (pred[16]{0:T(512)(128)(4,1)S(1)}, pred[16]{0:T(512)(128)(4,1)}, u32[]{:S(2)}) copy-start(pred[16]{0:T(512)(128)(4,1)} %get-tuple-element.21) | copy-start | bytes 52
  103.5 5.1 %copy-start.25 = (pred[16]{0:T(512)(128)(4,1)S(1)}, pred[16]{0:T(512)(128)(4,1)}, u32[]{:S(2)}) copy-start(pred[16]{0:T(512)(128)(4,1)} %get-tuple-element.22) | copy-start | bytes 52
  103.5 5.1 %copy-start.26 = (pred[16]{0:T(512)(128)(4,1)S(1)}, pred[16]{0:T(512)(128)(4,1)}, u32[]{:S(2)}) copy-start(pred[16]{0:T(512)(128)(4,1)} %get-tuple-element.23) | copy-start | bytes 52
  108.6 7.7 %copy-start.21 = (pred[16]{0:T(512)(128)(4,1)S(1)}, pred[16]{0:T(512)(128)(4,1)}, u32[]{:S(2)}) copy-start(pred[16]{0:T(512)(128)(4,1)} %get-tuple-element.15) | copy-start | bytes 52
  108.6 7.7 %copy-start.22 = (pred[16]{0:T(512)(128)(4,1)S(1)}, pred[16]{0:T(512)(128)(4,1)}, u32[]{:S(2)}) copy-start(pred[16]{0:T(512)(128)(4,1)} %get-tuple-element.18) | copy-start | bytes 52
  108.6 7.7 %copy-start.23 = (pred[16]{0:T(512)(128)(4,1)S(1)}, pred[16]{0:T(512)(128)(4,1)}, u32[]{:S(2)}) copy-start(pred[16]{0:T(512)(128)(4,1)} %get-tuple-element.20) | copy-start | bytes 52
  116.3 15.3 %copy-start.1 = (bf16[16,256,32]{1,2,0:T(8,128)(2,1)S(1)}, bf16[16,256,32]{1,2,0:T(8,128)(2,1)}, u32[]{:S(2)}) copy-start(bf16[16,256,32]{1,2,0:T(8,128)(2,1)} %param.15) | copy-start | bytes 786436
where the time goes:
time: 132 us
  matrix products  60.6 us (46%)
  blocking collectives  45.6 us (35%)
  other arithmetic  8.5 us (6%)
  local copies, waits for them, and re-layouts  8.28 us (6%)
  starting transfers between devices  7.96 us (6%)
    dot_general x3, matrix products, body(): jnp.einsum('npq,nqr->npr', chosen, shifted, preferred_element_type=jnp.fl...  30.5 us
    all_gather x1, blocking collectives, body(): lax.all_gather(couple_coarse, 'rhs', axis=0, tiled=True)  20.9 us
    all_gather x1, blocking collectives, body(): lax.all_gather(transfer_coarse, 'rhs', axis=0, tiled=True)  14.9 us
    dot_general x11, matrix products, couple_window(): jnp.einsum('nab,nbr->nar', chosen, shifted, preferred_element_type=jnp.fl...  12.8 us
    all_gather x1, blocking collectives, body(): whole = lax.all_gather(moments, 'rows', axis=0, tiled=True)  9.84 us
    ppermute x4, starting transfers between devices, padded_2(): lax.ppermute(head, axis, [((i + 1) % count, i) for i in range(count)])  7.22 us
    dot_general x1, matrix products, body(): jnp.einsum('npk,nkr->npr', target_basis, downward, preferred_element_type...  6.57 us
    concatenate x1, other arithmetic, padded_2(): jnp.concatenate([lax.ppermute(tail, axis, [(i, (i + 1) % count) for i in...  5.04 us
  transfers between devices with their start and end apart: 8, of which 0 were waited for; matrix products, arithmetic and copies ran while one was open for 35% of the time, Pallas kernels for 0%

commit v1 on v0

v1 whole, which is shorter than its diff:
```python
import jax
import jax.numpy as jnp
from jax import lax
from jax.experimental import pallas as pl
from jax.experimental.pallas import tpu as pltpu
from jax.sharding import PartitionSpec as P

MESH = pl.DeviceIdType.MESH
F32 = jnp.float32
BF16 = jnp.bfloat16


def dot(a, b):
    return lax.dot_general(a, b, (((1,), (0,)), ((), ())), preferred_element_type=F32)


def dot_t(a, b):
    return lax.dot_general(a, b, (((0,), (0,)), ((), ())), preferred_element_type=F32)


def kernel(
    dims,
    x_hbm,
    near_hbm,
    near_list,
    sb_hbm,
    tb_hbm,
    ef_hbm,
    ec_hbm,
    sf_hbm,
    sc_hbm,
    far_fine,
    far_coarse,
    out_hbm,
    xw,
    near,
    sb,
    tb,
    ef,
    ec,
    sf,
    sc,
    wf,
    wc,
    cw0,
    cw1,
    cw2,
    cw3,
    cr,
    cu,
    fr,
    f3,
    f2,
    f1,
    f0,
    part,
    obuf,
    load_sem,
    out_sem,
    halo_send,
    halo_recv,
    table_send,
    table_recv,
    gather_send,
    gather_recv,
):
    count, leaf, rank, R, T, chunks = dims
    me = lax.axis_index("rows")
    z = lax.axis_index("rhs")
    right, left = lax.rem(me + 1, R), lax.rem(me + R - 1, R)
    per = count // chunks
    block = ec.shape[0]

    loads = [
        pltpu.make_async_copy(ec_hbm, ec, load_sem.at[0]),
        pltpu.make_async_copy(sc_hbm, sc, load_sem.at[1]),
        pltpu.make_async_copy(sb_hbm, sb, load_sem.at[2]),
    ]
    x_loads = [
        pltpu.make_async_copy(
            x_hbm.at[pl.ds(c * per, per)], xw.at[pl.ds(1 + c * per, per)], load_sem.at[7 + c]
        )
        for c in range(chunks)
    ]
    late = [
        pltpu.make_async_copy(ef_hbm, ef, load_sem.at[3]),
        pltpu.make_async_copy(sf_hbm, sf, load_sem.at[4]),
        pltpu.make_async_copy(near_hbm, near, load_sem.at[5]),
        pltpu.make_async_copy(tb_hbm, tb, load_sem.at[6]),
    ]
    for copy in loads + x_loads + late:
        copy.start()

    barrier = pltpu.get_barrier_semaphore()
    for k in range(1, R):
        pl.semaphore_signal(
            barrier, inc=1, device_id=(lax.rem(me + k, R), z), device_id_type=MESH
        )
    for k in range(1, T):
        pl.semaphore_signal(
            barrier, inc=1, device_id=(me, lax.rem(z + k, T)), device_id_type=MESH
        )

    loads[0].wait()
    loads[1].wait()
    for r in range(block):
        wc[z * block + r] = jnp.concatenate([sc[r, 0], sc[r, 1], sc[r, 2], ec[r]], axis=1)
    pl.semaphore_wait(barrier, R + T - 2)

    def send(src, dst, send_sem, recv_sem, row, col):
        return pltpu.make_async_remote_copy(
            src_ref=src,
            dst_ref=dst,
            send_sem=send_sem,
            recv_sem=recv_sem,
            device_id=(row, col),
            device_id_type=MESH,
        )

    mine = wc.at[pl.ds(z * block, block)]
    tables = []
    for k in range(1, T):
        copy = send(
            mine, mine, table_send.at[k], table_recv.at[z], me, lax.rem(z + k, T)
        )
        copy.start()
        tables.append(copy)

    def halo(ref, width, size, level):
        low = send(
            ref.at[pl.ds(width, width)],
            ref.at[pl.ds(width + size, width)],
            halo_send.at[2 * level],
            halo_recv.at[2 * level],
            left,
            z,
        )
        high = send(
            ref.at[pl.ds(size, width)],
            ref.at[pl.ds(0, width)],
            halo_send.at[2 * level + 1],
            halo_recv.at[2 * level + 1],
            right,
            z,
        )
        low.start()
        high.start()
        return [low, high]

    loads[2].wait()
    for c in range(chunks):
        x_loads[c].wait()
        for t in range(c * per, (c + 1) * per):
            cw0[2 + t] = dot(sb[t], xw[1 + t]).astype(BF16)
    windows = [cw0, cw1, cw2, cw3]
    sizes = [count, count // 2, count // 4, count // 8]
    firsts = [0, count, count + count // 2]
    halos = [halo(cw0, 2, count, 0)]
    late[0].wait()
    for level in range(3):
        below, above = windows[level], windows[level + 1]
        for j in range(sizes[level + 1]):
            pair = below[2 + 2 * j : 4 + 2 * j].reshape(2 * rank, -1)
            first = firsts[level] + 2 * j
            matrix = ef[first : first + 2].reshape(2 * rank, rank)
            above[2 + j] = dot_t(matrix, pair).astype(BF16)
        halos.append(halo(above, 2, sizes[level + 1], level + 1))

    for k in range(1, T):
        other = lax.rem(z + k, T)
        theirs = wc.at[pl.ds(other * block, block)]
        send(theirs, theirs, table_send.at[k], table_recv.at[other], me, other).wait_recv()

    def transfer(row):
        return wc[row][:, 3 * rank :]

    own = dot_t(transfer(2 * R + 2 * me), cw3[2]) + dot_t(transfer(2 * R + 2 * me + 1), cw3[3])
    cr[me] = own.astype(BF16)
    gathers = []
    for k in range(1, R):
        spot = cr.at[pl.ds(me, 1)]
        copy = send(
            spot, spot, gather_send.at[k], gather_recv.at[me], lax.rem(me + k, R), z
        )
        copy.start()
        gathers.append(copy)
    halos.append(halo(xw, 1, count, 4))

    late[1].wait()
    for j in range(wf.shape[0]):
        wf[j] = jnp.concatenate([sf[j, 0], sf[j, 1], sf[j, 2], ef[j]], axis=1)

    total = count * R
    late[2].wait()

    def near_leaf(t):
        total_sum = None
        for wanted in (-1, 0, 1):
            target = lax.rem(me * count + t + wanted + total, total)
            slot = jnp.where(
                near_list[0, t] == target, 0, jnp.where(near_list[1, t] == target, 1, 2)
            )
            term = dot(near[t, slot], xw[1 + t + wanted])
            total_sum = term if total_sum is None else total_sum + term
        return total_sum

    def near_step(i, carry):
        for u in range(2):
            t = 1 + 2 * i + u
            part[t] = near_leaf(t)
        return carry

    lax.fori_loop(0, (count - 2) // 2, near_step, 0)

    for k in range(1, R):
        other = lax.rem(me + k, R)
        spot = cr.at[pl.ds(other, 1)]
        send(spot, spot, gather_send.at[k], gather_recv.at[other], other, z).wait_recv()

    def coarse(n, index):
        return cr[index] if n == R else cu[n - 4 + index]

    n = R // 2
    while n >= 4:
        for j in range(n):
            lifted = dot_t(transfer(2 * n + 2 * j), coarse(2 * n, 2 * j)) + dot_t(
                transfer(2 * n + 2 * j + 1), coarse(2 * n, 2 * j + 1)
            )
            cu[n - 4 + j] = lifted.astype(BF16)
        n //= 2
    n = 4
    value = None
    while n <= R:
        row = n + me // (R // n)
        if n == 4:
            value = dot(wc[row][:, :rank], coarse(n, far_coarse[0, row]))
        else:
            parts = [coarse(n, far_coarse[s, row]) for s in range(3)] + [value]
            value = dot(wc[row], jnp.concatenate(parts, axis=0))
        value = value.astype(BF16)
        n *= 2
    fr[0] = value

    def wait_halo(level):
        for copy in halos[level]:
            copy.wait_recv()

    wait_halo(3)
    for i in range(2):
        row = 2 * R + 2 * me + i
        parts = [
            cw3[jnp.minimum(lax.rem(far_coarse[s, row] - 2 * me + 2 + 2 * R, 2 * R), 5)]
            for s in range(3)
        ] + [fr[0]]
        f3[i] = dot(wc[row], jnp.concatenate(parts, axis=0)).astype(BF16)
    above = f3
    for level, below in ((2, f2), (1, f1), (0, f0)):
        wait_halo(level)
        m = sizes[level]
        n = m * R
        for i in range(m):
            row = firsts[level] + i
            parts = [
                windows[level][jnp.minimum(lax.rem(far_fine[s, row] - m * me + 2 + n, n), m + 3)]
                for s in range(3)
            ] + [above[i // 2]]
            below[i] = dot(wf[row], jnp.concatenate(parts, axis=0)).astype(BF16)
        above = below

    late[3].wait()
    wait_halo(4)
    part[0] = near_leaf(0)
    part[count - 1] = near_leaf(count - 1)
    stores = []
    for c in range(chunks):
        for t in range(c * per, (c + 1) * per):
            obuf[t] = (part[t] + dot_t(tb[t], f0[t])).astype(BF16)
        copy = pltpu.make_async_copy(
            obuf.at[pl.ds(c * per, per)], out_hbm.at[pl.ds(c * per, per)], out_sem.at[c]
        )
        copy.start()
        stores.append(copy)
    for copy in tables + gathers:
        copy.wait_send()
    for pair in halos:
        for copy in pair:
            copy.wait_send()
    for copy in stores:
        copy.wait()


def body(
    sources,
    near_blocks,
    near_list,
    source_basis,
    target_basis,
    transfer_fine,
    transfer_coarse,
    couple_fine,
    couple_coarse,
    far_fine,
    far_coarse,
):
    count, _, leaf, _ = near_blocks.shape
    rank = source_basis.shape[2]
    width = sources.shape[1]
    R, T = lax.axis_size("rows"), lax.axis_size("rhs")
    fine = transfer_fine.shape[0]
    block = transfer_coarse.shape[0]
    chunks = 4
    dims = (count, leaf, rank, R, T, chunks)
    anyspace = pl.BlockSpec(memory_space=pl.ANY)
    smem = pl.BlockSpec(memory_space=pltpu.SMEM)

    def moments(clusters):
        return pltpu.VMEM((clusters, rank, width), BF16)

    out = pl.pallas_call(
        lambda *refs: kernel(dims, *refs),
        name="tree_apply",
        out_shape=jax.ShapeDtypeStruct((count, leaf, width), BF16),
        in_specs=[
            anyspace,
            anyspace,
            smem,
            anyspace,
            anyspace,
            anyspace,
            anyspace,
            anyspace,
            anyspace,
            smem,
            smem,
        ],
        out_specs=anyspace,
        scratch_shapes=[
            pltpu.VMEM((count + 2, leaf, width), BF16),
            pltpu.VMEM(near_blocks.shape, BF16),
            pltpu.VMEM((count, rank, leaf), BF16),
            pltpu.VMEM((count, rank, leaf), BF16),
            pltpu.VMEM(transfer_fine.shape, BF16),
            pltpu.VMEM(transfer_coarse.shape, BF16),
            pltpu.VMEM(couple_fine.shape, BF16),
            pltpu.VMEM(couple_coarse.shape, BF16),
            pltpu.VMEM((fine, rank, 4 * rank), BF16),
            pltpu.VMEM((block * T, rank, 4 * rank), BF16),
            moments(count + 4),
            moments(count // 2 + 4),
            moments(count // 4 + 4),
            moments(count // 8 + 4),
            moments(R),
            moments(R),
            moments(1),
            moments(count // 8),
            moments(count // 4),
            moments(count // 2),
            moments(count),
            pltpu.VMEM((count, leaf, width), F32),
            pltpu.VMEM((count, leaf, width), BF16),
            pltpu.SemaphoreType.DMA((7 + chunks,)),
            pltpu.SemaphoreType.DMA((chunks,)),
            pltpu.SemaphoreType.DMA((10,)),
            pltpu.SemaphoreType.DMA((10,)),
            pltpu.SemaphoreType.DMA((T,)),
            pltpu.SemaphoreType.DMA((T,)),
            pltpu.SemaphoreType.DMA((R,)),
            pltpu.SemaphoreType.DMA((R,)),
        ],
        compiler_params=pltpu.CompilerParams(
            collective_id=0, has_side_effects=True, vmem_limit_bytes=56 * 1024 * 1024
        ),
    )(
        sources.reshape(count, leaf, width),
        near_blocks,
        near_list.T,
        jnp.swapaxes(source_basis, 1, 2),
        jnp.swapaxes(target_basis, 1, 2),
        transfer_fine,
        transfer_coarse,
        couple_fine,
        couple_coarse,
        far_fine.T,
        far_coarse.T,
    )
    return out.reshape(count * leaf, width)


def solution(mesh):
    in_specs = (
        P("rows", "rhs"),
        P("rows", None, None, None),
        P("rows", None),
        P("rows", None, None),
        P("rows", None, None),
        P("rows", None, None),
        P("rhs", None, None),
        P("rows", None, None, None),
        P("rhs", None, None, None),
        P("rows", None),
        P(),
    )
    out_specs = P("rows", "rhs")
    return jax.shard_map(body, mesh=mesh, in_specs=in_specs, out_specs=out_specs, check_vma=False)
```

time: 132 us -> 30.8 us (0.23)
  matrix products: 60.6 us -> 0 us
  blocking collectives: 45.6 us -> 0 us
  Pallas kernels: 0 us -> 26.1 us
  other arithmetic: 8.5 us -> 0 us
  starting transfers between devices: 7.96 us -> 0 us
  local copies, waits for them, and re-layouts: 8.28 us -> 4.47 us
    dot_general x29 -> x0, matrix products: 60.6 us -> none  [the longest x3 30.5 us: body(): jnp.einsum('npq,nqr->npr', chosen, shifted, preferred_element_type=jnp.fl...]
    all_gather x3 -> x0, blocking collectives: 45.6 us -> none  [the longest x1 20.9 us: body(): lax.all_gather(couple_coarse, 'rhs', axis=0, tiled=True)]
    pallas_call x0 -> x1, Pallas kernels: none -> 26.1 us  [body(): pl.pallas_call(lambda *refs: kernel(dims, *refs), name='tree_apply', out_...]
    ppermute x8 -> x0, starting transfers between devices: 7.96 us -> none  [the longest x4 7.22 us: padded_2(): lax.ppermute(head, axis, [((i + 1) % count, i) for i in range(count)])]
    concatenate x1 -> x0, other arithmetic: 5.04 us -> none  [padded_2(): jnp.concatenate([lax.ppermute(tail, axis, [(i, (i + 1) % count) for i in...]
    unnamed x60 -> x1, local copies, waits for them, and re-layouts: 0.13 us -> 4.47 us
    slice x4 -> x0, local copies, waits for them, and re-layouts: 4 us -> none  [the longest x3 2.11 us: padded_2(): lax.slice_in_dim(cells, cells.shape[dim] - width, cells.shape[dim], axis=...]
    gather x3 -> x0, local copies, waits for them, and re-layouts: 2.6 us -> none  [couple_masked(): picked = moments[jnp.maximum(partners, 0)]]
  transfers between devices with their start and end apart: 8 -> 0, of which waited for: 0 -> 0; matrix products, arithmetic and copies ran while one was open for 35% -> 0% of each run, Pallas kernels for 0% -> 0%
where the time goes in v1:
time: 30.8 us; the launch traced here: 30.6 us
  Pallas kernels  26.1 us (85%)
  local copies, waits for them, and re-layouts  4.47 us (15%)
    pallas_call x1, Pallas kernels, body(): pl.pallas_call(lambda *refs: kernel(dims, *refs), name='tree_apply', out_...  26.1 us
    unnamed x1, local copies, waits for them, and re-layouts  4.47 us

profile of v1, /device:TPU:0, one launch (start us, length us, event | category | flops | bytes accessed | tf_op | source)
XLA Modules:
  0.0 30.6 jit_solution(7100359562908831959)
XLA Ops:
  0.0 26.1 %tree_apply.1 = bf16[16,256,512]{2,1,0:T(8,128)(2,1)} custom-call(bf16[16,256,512]{2,1,0:T(8,128)(2,1)} %bitcast.8, bf16[16,3,256,256]{3,2,1,0:T(8,128)(2,1)} %refs_1_.1, s32[3,16]{1,0:T(4,128)} %bitcast.11, bf16[16,32,256]{2,1,0:T(8,128)(2,1)} %bitcast.9, bf16[16,32,256]{2,1,0:T(8,128)(2,1)} %bitcast.10, bf16[28,32,32]{2,1,0:T(8,128)(2,1)} %refs_5_.1, ...), custom_call_target="tpu_custom_call" | custom-call | tf_op jit(solution)/shard_map/tree_apply/pallas_call | solution.py:319
  26.2 4.5 %copy.13 = bf16[4096,512]{1,0:T(8,128)(2,1)} copy(bf16[4096,512]{1,0:T(8,128)(2,1)} %bitcast.7) | data formatting | bytes 8388608

commit v2 on v1

--- a/solution.py
+++ b/solution.py
@@ -24,18 +24,17 @@
     near_hbm,
     near_list,
     sb_hbm,
-    tb_hbm,
     ef_hbm,
     ec_hbm,
     sf_hbm,
     sc_hbm,
     far_fine,
     far_coarse,
-    out_hbm,
+    part_hbm,
+    f_hbm,
     xw,
     near,
     sb,
-    tb,
     ef,
     ec,
     sf,
@@ -54,7 +53,6 @@
     f1,
     f0,
     part,
-    obuf,
     load_sem,
     out_sem,
     halo_send,
@@ -63,6 +61,8 @@
     table_recv,
     gather_send,
     gather_recv,
+    pair_send,
+    pair_recv,
 ):
     count, leaf, rank, R, T, chunks = dims
     me = lax.axis_index("rows")
@@ -86,9 +86,8 @@
         pltpu.make_async_copy(ef_hbm, ef, load_sem.at[3]),
         pltpu.make_async_copy(sf_hbm, sf, load_sem.at[4]),
         pltpu.make_async_copy(near_hbm, near, load_sem.at[5]),
-        pltpu.make_async_copy(tb_hbm, tb, load_sem.at[6]),
     ]
-    for copy in loads + x_loads + late:
+    for copy in loads + x_loads + late[:2]:
         copy.start()
 
     barrier = pltpu.get_barrier_semaphore()
@@ -117,14 +116,46 @@
             device_id_type=MESH,
         )
 
+    low = send(
+        x_hbm.at[pl.ds(0, 1)],
+        xw.at[pl.ds(count + 1, 1)],
+        halo_send.at[8],
+        halo_recv.at[8],
+        left,
+        z,
+    )
+    high = send(
+        x_hbm.at[pl.ds(count - 1, 1)],
+        xw.at[pl.ds(0, 1)],
+        halo_send.at[9],
+        halo_recv.at[9],
+        right,
+        z,
+    )
+    low.start()
+    high.start()
+    edges = [low, high]
+
+    pair_rows = wc.at[pl.ds(2 * R + 2 * me, 2)]
+    pair_owner = (2 * R + 2 * me) // block
+    coarse_blocks = (2 * R + block - 1) // block
     mine = wc.at[pl.ds(z * block, block)]
-    tables = []
-    for k in range(1, T):
-        copy = send(
-            mine, mine, table_send.at[k], table_recv.at[z], me, lax.rem(z + k, T)
-        )
-        copy.start()
-        tables.append(copy)
+
+    def pair_copy(k, source, target):
+        return send(pair_rows, pair_rows, pair_send.at[k], pair_recv.at[source], me, target)
+
+    def table_copy(k, source, target):
+        return send(mine, mine, table_send.at[k], table_recv.at[source], me, target)
+
+    @pl.when(z == pair_owner)
+    def _():
+        for k in range(1, T):
+            pair_copy(k, z, lax.rem(z + k, T)).start()
+
+    @pl.when(z < coarse_blocks)
+    def _():
+        for k in range(1, T):
+            table_copy(k, z, lax.rem(z + k, T)).start()
 
     def halo(ref, width, size, level):
         low = send(
@@ -150,12 +181,13 @@
     loads[2].wait()
     for c in range(chunks):
         x_loads[c].wait()
+    late[2].start()
+    for c in range(chunks):
         for t in range(c * per, (c + 1) * per):
             cw0[2 + t] = dot(sb[t], xw[1 + t]).astype(BF16)
     windows = [cw0, cw1, cw2, cw3]
     sizes = [count, count // 2, count // 4, count // 8]
     firsts = [0, count, count + count // 2]
-    halos = [halo(cw0, 2, count, 0)]
     late[0].wait()
     for level in range(3):
         below, above = windows[level], windows[level + 1]
@@ -164,12 +196,10 @@
             first = firsts[level] + 2 * j
             matrix = ef[first : first + 2].reshape(2 * rank, rank)
             above[2 + j] = dot_t(matrix, pair).astype(BF16)
-        halos.append(halo(above, 2, sizes[level + 1], level + 1))
-
-    for k in range(1, T):
-        other = lax.rem(z + k, T)
-        theirs = wc.at[pl.ds(other * block, block)]
-        send(theirs, theirs, table_send.at[k], table_recv.at[other], me, other).wait_recv()
+
+    @pl.when(z != pair_owner)
+    def _():
+        pair_copy(0, pair_owner, lax.rem(z + 1, T)).wait_recv()
 
     def transfer(row):
         return wc[row][:, 3 * rank :]
@@ -184,7 +214,9 @@
         )
         copy.start()
         gathers.append(copy)
-    halos.append(halo(xw, 1, count, 4))
+    halos = [None] * 4
+    for level in (3, 2, 1, 0):
+        halos[level] = halo(windows[level], 2, sizes[level], level)
 
     late[1].wait()
     for j in range(wf.shape[0]):
@@ -207,15 +239,39 @@
     def near_step(i, carry):
         for u in range(2):
             t = 1 + 2 * i + u
-            part[t] = near_leaf(t)
+            part[t] = near_leaf(t).astype(BF16)
         return carry
 
     lax.fori_loop(0, (count - 2) // 2, near_step, 0)
+    stores = [
+        pltpu.make_async_copy(
+            part.at[pl.ds(1, count - 2)], part_hbm.at[pl.ds(1, count - 2)], out_sem.at[0]
+        ),
+        pltpu.make_async_copy(part.at[pl.ds(0, 1)], part_hbm.at[pl.ds(0, 1)], out_sem.at[1]),
+        pltpu.make_async_copy(
+            part.at[pl.ds(count - 1, 1)], part_hbm.at[pl.ds(count - 1, 1)], out_sem.at[2]
+        ),
+    ]
+    stores[0].start()
+    edges[0].wait_recv()
+    part[count - 1] = near_leaf(count - 1).astype(BF16)
+    edges[1].wait_recv()
+    part[0] = near_leaf(0).astype(BF16)
+    stores[1].start()
+    stores[2].start()
 
     for k in range(1, R):
         other = lax.rem(me + k, R)
         spot = cr.at[pl.ds(other, 1)]
         send(spot, spot, gather_send.at[k], gather_recv.at[other], other, z).wait_recv()
+
+    for k in range(1, T):
+        other = lax.rem(z + k, T)
+        theirs = wc.at[pl.ds(other * block, block)]
+
+        @pl.when(other < coarse_blocks)
+        def _():
+            send(theirs, theirs, table_send.at[0], table_recv.at[other], me, other).wait_recv()
 
     def coarse(n, index):
         return cr[index] if n == R else cu[n - 4 + index]
@@ -267,26 +323,32 @@
             below[i] = dot(wf[row], jnp.concatenate(parts, axis=0)).astype(BF16)
         above = below
 
-    late[3].wait()
-    wait_halo(4)
-    part[0] = near_leaf(0)
-    part[count - 1] = near_leaf(count - 1)
-    stores = []
-    for c in range(chunks):
-        for t in range(c * per, (c + 1) * per):
-            obuf[t] = (part[t] + dot_t(tb[t], f0[t])).astype(BF16)
-        copy = pltpu.make_async_copy(
-            obuf.at[pl.ds(c * per, per)], out_hbm.at[pl.ds(c * per, per)], out_sem.at[c]
-        )
-        copy.start()
-        stores.append(copy)
-    for copy in tables + gathers:
+    last = pltpu.make_async_copy(f0, f_hbm, out_sem.at[3])
+    last.start()
+
+    @pl.when(z == pair_owner)
+    def _():
+        for k in range(1, T):
+            pair_copy(k, z, lax.rem(z + k, T)).wait_send()
+
+    @pl.when(z < coarse_blocks)
+    def _():
+        for k in range(1, T):
+            table_copy(k, z, lax.rem(z + k, T)).wait_send()
+
+    for copy in gathers + edges:
         copy.wait_send()
     for pair in halos:
         for copy in pair:
             copy.wait_send()
     for copy in stores:
         copy.wait()
+    last.wait()
+
+
+def finish(part, tb, f, out):
+    for t in range(part.shape[0]):
+        out[t] = (part[t].astype(F32) + dot_t(tb[t], f[t])).astype(BF16)
 
 
 def body(
@@ -316,28 +378,18 @@
     def moments(clusters):
         return pltpu.VMEM((clusters, rank, width), BF16)
 
-    out = pl.pallas_call(
+    part, far = pl.pallas_call(
         lambda *refs: kernel(dims, *refs),
         name="tree_apply",
-        out_shape=jax.ShapeDtypeStruct((count, leaf, width), BF16),
-        in_specs=[
-            anyspace,
-            anyspace,
-            smem,
-            anyspace,
-            anyspace,
-            anyspace,
-            anyspace,
-            anyspace,
-            anyspace,
-            smem,
-            smem,
+        out_shape=[
+            jax.ShapeDtypeStruct((count, leaf, width), BF16),
+            jax.ShapeDtypeStruct((count, rank, width), BF16),
         ],
-        out_specs=anyspace,
+        in_specs=[anyspace] * 2 + [smem] + [anyspace] * 5 + [smem] * 2,
+        out_specs=[anyspace, anyspace],
         scratch_shapes=[
             pltpu.VMEM((count + 2, leaf, width), BF16),
             pltpu.VMEM(near_blocks.shape, BF16),
-            pltpu.VMEM((count, rank, leaf), BF16),
             pltpu.VMEM((count, rank, leaf), BF16),
             pltpu.VMEM(transfer_fine.shape, BF16),
             pltpu.VMEM(transfer_coarse.shape, BF16),
@@ -356,26 +408,26 @@
             moments(count // 4),
             moments(count // 2),
             moments(count),
-            pltpu.VMEM((count, leaf, width), F32),
             pltpu.VMEM((count, leaf, width), BF16),
             pltpu.SemaphoreType.DMA((7 + chunks,)),
-            pltpu.SemaphoreType.DMA((chunks,)),
+            pltpu.SemaphoreType.DMA((4,)),
             pltpu.SemaphoreType.DMA((10,)),
             pltpu.SemaphoreType.DMA((10,)),
             pltpu.SemaphoreType.DMA((T,)),
             pltpu.SemaphoreType.DMA((T,)),
             pltpu.SemaphoreType.DMA((R,)),
             pltpu.SemaphoreType.DMA((R,)),
+            pltpu.SemaphoreType.DMA((T,)),
+            pltpu.SemaphoreType.DMA((T,)),
         ],
         compiler_params=pltpu.CompilerParams(
-            collective_id=0, has_side_effects=True, vmem_limit_bytes=56 * 1024 * 1024
+            collective_id=0, has_side_effects=True, vmem_limit_bytes=63 * 1024 * 1024
         ),
     )(
         sources.reshape(count, leaf, width),
         near_blocks,
         near_list.T,
         jnp.swapaxes(source_basis, 1, 2),
-        jnp.swapaxes(target_basis, 1, 2),
         transfer_fine,
         transfer_coarse,
         couple_fine,
@@ -383,6 +435,17 @@
         far_fine.T,
         far_coarse.T,
     )
+    step = 4
+    block_of = lambda *tail: pl.BlockSpec((step,) + tail, lambda i: (i, 0, 0))
+    out = pl.pallas_call(
+        finish,
+        name="far_add",
+        grid=(count // step,),
+        out_shape=jax.ShapeDtypeStruct((count, leaf, width), BF16),
+        in_specs=[block_of(leaf, width), block_of(rank, leaf), block_of(rank, width)],
+        out_specs=block_of(leaf, width),
+        compiler_params=pltpu.CompilerParams(vmem_limit_bytes=63 * 1024 * 1024),
+    )(part, jnp.swapaxes(target_basis, 1, 2), far)
     return out.reshape(count * leaf, width)
 
 

time: 30.8 us -> 29.6 us (0.961)
  local copies, waits for them, and re-layouts: 4.47 us -> 0 us
  Pallas kernels: 26.1 us -> 29.4 us
    pallas_call x0 -> x1, Pallas kernels: none -> 5.69 us  [body(): pl.pallas_call(finish, name='far_add', grid=(count // step,), out_shape=j...]
    unnamed x1 -> x0, local copies, waits for them, and re-layouts: 4.47 us -> none
    pallas_call x1, Pallas kernels: 26.1 us -> 23.7 us  [body(): pl.pallas_call(lambda *refs: kernel(dims, *refs), name='tree_apply', out_...]
where the time goes in v2:
time: 29.6 us; the launch traced here: 29.4 us
  Pallas kernels  29.4 us (99%)
    pallas_call x1, Pallas kernels, body(): pl.pallas_call(lambda *refs: kernel(dims, *refs), name='tree_apply', out_...  23.7 us
    pallas_call x1, Pallas kernels, body(): pl.pallas_call(finish, name='far_add', grid=(count // step,), out_shape=j...  5.69 us

profile of v2, /device:TPU:0, one launch (start us, length us, event | category | flops | bytes accessed | tf_op | source)
XLA Modules:
  0.0 29.4 jit_solution(8771028041910363492)
XLA Ops:
  0.0 23.7 %tree_apply.1 = (bf16[16,256,512]{2,1,0:T(8,128)(2,1)}, bf16[16,32,512]{2,1,0:T(8,128)(2,1)}) custom-call(bf16[16,256,512]{2,1,0:T(8,128)(2,1)} %bitcast.7, bf16[16,3,256,256]{3,2,1,0:T(8,128)(2,1)} %refs_1_.1, s32[3,16]{1,0:T(4,128)} %bitcast.10, bf16[16,32,256]{2,1,0:T(8,128)(2,1)} %bitcast.8, bf16[28,32,32]{2,1,0:T(8,128)(2,1)} %refs_4_.1, ...), custom_call_target="tpu_custom_call" | custom-call | tf_op jit(solution)/shard_map/tree_apply/pallas_call | solution.py:381
  23.7 5.7 %far_add.1 = bf16[16,256,512]{2,1,0:T(8,128)(2,1)} custom-call(bf16[16,256,512]{2,1,0:T(8,128)(2,1)} %get-tuple-element.7.part, bf16[16,32,256]{2,1,0:T(8,128)(2,1)} %bitcast.9, bf16[16,32,512]{2,1,0:T(8,128)(2,1)} %get-tuple-element.8.f), custom_call_target="tpu_custom_call" | custom-call | tf_op jit(solution)/shard_map/far_add/pallas_call | solution.py:440
